TPU v7x, 256 devices: a whole 4x4x8 slice. The times are simulated.
256 devices in a mesh: dp: 16 (over y_hi, x, core), seq: 16 (over y_lo, z).
Axes of the slice: x: 4, y: 4 (y_hi: 2, y_lo: 2; y = y_hi * 2 + y_lo), z: 8, core: 2. Of those that a mesh axis runs over, the one named last changes fastest.
Arguments:
- tokens: bfloat16 [16, 4096, 1280], P('dp', 'seq'), may hold values from -6 to 6
- tube_index: int32 [16, 4096], P('dp', 'seq'), may hold values from 0 to 16383
- counts: int32 [16, 16], P('dp', 'seq'), may hold values from 128 to 256
- qkv_weight: bfloat16 [1280, 3840], P('dp'), may hold values from -4 to 4
- proj_weight: bfloat16 [1280, 1280], P('dp'), may hold values from -0.15625 to 0.15625
- ctx_b: bfloat16 [16, 4096, 1280], P('dp', 'seq'), may hold values from -12 to 12
- cot_b: bfloat16 [16, 4096, 1280], P('dp', 'seq'), may hold values from -12 to 12
- b_counts: int32 [16, 16], P('dp', 'seq'), may hold values from 128 to 256
Outputs:
- out_a: bfloat16 [16, 4096, 1280], P('dp', 'seq')
- weight_grad: float32 [1280, 1280], P('dp')
Inputs may be any that keep to these rules, and one draw needn't show every extreme that they name: `counts`: slots of a device's block past its count hold padding. `b_counts`: slots of a device's block past its count hold padding.
All inputs are finite; a program needn't handle non-finite values.
Results may differ from a plain program's by a relative error of at most 0.017.
Values may be sent and summed in bfloat16 or wider, within the bound.
No kernel may reach another device: no remote copies, remote signals or barrier semaphores. Data moves between devices by JAX's collectives and lax.ppermute only.
A program may use at most 128 MiB of HBM per device.

v0:
```python
import math
import jax
import jax.numpy as jnp
from jax import lax
from jax.sharding import Mesh
from jax.sharding import PartitionSpec as P

HEADS = 16
SEQ = ("seq_0", "seq_1")
DP = ("dp_0", "dp_1", "dp_2")


def in_order(parts, dim):
    shape = list(parts.shape[1:])
    shape[dim] *= parts.shape[0]
    return jnp.moveaxis(parts, 0, dim).reshape(shape)


def stacked_from(x, axes, sequence):
    parts = x
    for k in sequence:
        parts = lax.all_gather(parts, axes[k])
    done = sequence[::-1]
    back = [done.index(k) for k in range(len(axes))]
    parts = parts.transpose(*back, *range(len(axes), parts.ndim))
    return parts.reshape(-1, *x.shape)


def gathered_by_axis(x, axes, sequence, dim):
    return in_order(stacked_from(x, axes, sequence), dim)


def over_pieces(x, axis):
    return lax.all_gather(x, axis).astype(jnp.float32).sum(0)


def embed(tube_ids, model_width):
    half_width = model_width // 2
    positions = jnp.arange(half_width, dtype=jnp.float32)
    frequency = jnp.exp(positions * (-2.0 * math.log(10000.0) / model_width))
    angles = tube_ids.astype(jnp.float32)[:, None] * frequency[None, :]
    return jnp.concatenate([jnp.sin(angles), jnp.cos(angles)], axis=1)


def layer_norm(values):
    centered = values - jnp.mean(values, axis=1, keepdims=True)
    spread = jnp.mean(centered * centered, axis=1, keepdims=True)
    return centered * lax.rsqrt(spread + 1e-06)


def attend(grouped, valid_keys, heads_here, head_width):
    seq_length = grouped.shape[0]
    query_rows = grouped[:, 0].reshape(seq_length, heads_here, head_width)
    key_rows = grouped[:, 1].reshape(seq_length, heads_here, head_width)
    value_rows = grouped[:, 2].reshape(seq_length, heads_here, head_width)
    block_rows = math.gcd(seq_length, 512)
    score_scale = 1.0 / math.sqrt(head_width)
    blocked = query_rows.reshape(seq_length // block_rows, block_rows, heads_here, head_width)

    def one_block(block_query):
        scores = (
            jnp.einsum("qhd,khd->hqk", block_query, key_rows, preferred_element_type=jnp.float32)
            * score_scale
        )
        scores = jnp.where(valid_keys[None, None, :], scores, -1e30)
        top_score = jnp.max(scores, axis=2, keepdims=True)
        exponent = jnp.exp(scores - top_score)
        weights = (exponent / jnp.sum(exponent, axis=2, keepdims=True)).astype(jnp.bfloat16)
        return jnp.einsum(
            "hqk,khd->qhd", weights, value_rows, preferred_element_type=jnp.float32
        ).astype(jnp.bfloat16)

    return lax.map(one_block, blocked).reshape(seq_length, heads_here * head_width)


def on_device(tokens, tube_index, counts, qkv_weight, proj_weight, ctx_b, cot_b, b_counts):
    slot_cap = tokens.shape[1]
    model_width = tokens.shape[2]
    seq_count = lax.axis_size(SEQ)
    dp_count = lax.axis_size(DP)
    heads_here = HEADS // seq_count
    head_width = model_width // HEADS
    with_pos = tokens[0].astype(jnp.float32) + embed(tube_index[0], model_width)
    normed = layer_norm(with_pos).astype(jnp.bfloat16)
    columns = normed
    projected = jnp.dot(
        columns,
        lax.all_gather(qkv_weight, DP, axis=0, tiled=True),
        preferred_element_type=jnp.float32,
    ).astype(jnp.bfloat16)
    all_counts = gathered_by_axis(counts, SEQ, (0, 1), 1)
    slot_ids = lax.broadcasted_iota(jnp.int32, (1, slot_cap), 1)
    valid_keys = (slot_ids < all_counts[0][:, None]).reshape(seq_count * slot_cap)
    grouped = lax.all_to_all(
        projected.reshape(slot_cap, 3, model_width), SEQ, split_axis=2, concat_axis=0, tiled=True
    )
    head_context = attend(grouped, valid_keys, heads_here, head_width)
    context = lax.all_to_all(head_context, SEQ, split_axis=0, concat_axis=1, tiled=True)
    columns = context
    mixed = jnp.dot(
        columns, gathered_by_axis(proj_weight, DP, (0, 1, 2), 0), preferred_element_type=jnp.float32
    )
    out_a = (with_pos + mixed).astype(jnp.bfloat16)[None]
    row_ids = lax.broadcasted_iota(jnp.int32, (slot_cap, 1), 0)
    keep_rows = row_ids < b_counts[0, 0]
    masked_cot = jnp.where(keep_rows, cot_b[0], jnp.zeros((), jnp.bfloat16))
    factor = 1.0 / math.sqrt(dp_count * seq_count * slot_cap)
    column_part = ctx_b[0]
    own_rows = lax.psum_scatter(
        lax.dot_general(
            column_part, masked_cot, (((0,), (0,)), ((), ())), preferred_element_type=jnp.float32
        )
        * factor,
        DP,
        scatter_dimension=0,
        tiled=True,
    )
    weight_grad = over_pieces(own_rows.astype(jnp.bfloat16), SEQ).astype(jnp.float32)
    return (out_a, weight_grad)


def solution(mesh):
    split = Mesh(mesh.devices.reshape(2, 4, 2, 2, 8), ("dp_0", "dp_1", "dp_2", "seq_0", "seq_1"))
    return jax.shard_map(
        on_device,
        mesh=split,
        in_specs=(
            P(DP, SEQ, None),
            P(DP, SEQ),
            P(DP, SEQ),
            P(DP, None),
            P(DP, None),
            P(DP, SEQ, None),
            P(DP, SEQ, None),
            P(DP, SEQ),
        ),
        out_specs=(P(DP, SEQ, None), P(DP, None)),
        check_vma=False,
    )
```

profile of v0, /device:TPU:4, one launch (start us, length us, event | category | flops | bytes accessed | tf_op | source)
XLA Modules:
  0.0 355.5 jit_solution(13332053079246862315)
XLA Ops:
  7.2 0.7 all-gather.11.cloned.1.call-update
  8.0 10.9 %all-gather.2 = bf16[160,1280]{1,0:T(8,128)(2,1)} all-gather(bf16[80,1280]{1,0:T(8,128)(2,1)} %param.14), channel_id=4, replica_groups=mesh['dp_0'=2,'dp_1'=4,'dp_2'=2,'seq_0'=2,'seq_1'=8] {'dp_0'}, dimensions={0}, use_global_device_ids=true | all-gather | bytes 614400 | tf_op jit(solution)/shard_map/all_gather | solution.py:22
  19.6 5.0 %fusion.16 = f32[1280,1280]{0,1:T(8,128)} fusion(bf16[1,256,1280]{2,1,0:T(8,128)(2,1)S(1)} %copy-done, bf16[1,256,1280]{2,1,0:T(8,128)(2,1)} %param.16, pred[256]{0:T(512)(128)(4,1)S(1)} %iota_compare_fusion.1), kind=kOutput, calls=%fused_computation.20 | convolution fusion | flops 840826880 | bytes 7864576 | tf_op jit(solution)/shard_map/dot_general | solution.py:110
  24.6 8.3 %copy.45 = f32[1280,1280]{1,0:T(8,128)} copy(f32[1280,1280]{0,1:T(8,128)} %fusion.16) | data formatting | bytes 13107200
  32.9 0.7 copy-done.9
  33.5 2.3 multiply_sine_fusion
  36.5 59.3 %all-gather.11.cloned.1.call-done = bf16[1280,3840]{1,0:T(8,128)(2,1)} async-done(((bf16[80,3840]{1,0:T(8,128)(2,1)}), bf16[1280,3840]{1,0:T(8,128)(2,1)}) %all-gather.11.cloned.1.call-update) | async-done | bytes 9830416 | tf_op jit(solution)/shard_map/all_gather | solution.py:88
  95.8 7.9 %convolution_convert_fusion = bf16[256,3840]{1,0:T(8,128)(2,1)} fusion(bf16[1280,3840]{1,0:T(8,128)(2,1)} %all-gather.11.cloned.1.call-done, f32[256]{0:T(256)S(1)} %add_rsqrt_fusion, f32[256]{0:T(256)S(1)} %broadcast_multiply_fusion, f32[256,640]{1,0:T(8,128)S(1)} %get-tuple-element.86, f32[256,640]{1,0:T(8,128)S(1)} %get-tuple-element.85, ...), kind=kOutput, calls=%fused_computation.22 | convolution fusion | flops 2519531520 | bytes 13764608 | tf_op jit(solution)/shard_map/dot_general | solution.py:86
  103.6 2.7 copy.35
  106.3 11.2 %copy.36 = bf16[256,3,1280]{0,1,2:T(4,128)(2,1)} copy(bf16[256,3,1280]{0,2,1:T(8,128)(2,1)S(1)} %bitcast.93) | data formatting | bytes 3932160 | tf_op jit(solution)/shard_map/reshape | solution.py:95
  117.6 7.3 %all-to-all-start = ((bf16[256,3,1280]{0,1,2:T(4,128)(2,1)}), bf16[256,3,1280]{0,1,2:T(4,128)(2,1)S(1)}, u32[]{:S(2)}, u32[]{:S(2)}) async-start(bf16[256,3,1280]{0,1,2:T(4,128)(2,1)} %copy.36), calls=%async_computation | async-start | bytes 5242880 | tf_op jit(solution)/shard_map/all_to_all | solution.py:94
  126.7 0.9 bitcast_dynamic-update-slice_fusion
  127.6 4.5 %all-reduce = s32[2]{0:T(128)S(1)} all-reduce(s32[2]{0:T(128)S(1)} %bitcast_dynamic-update-slice_fusion), channel_id=2, replica_groups=mesh['dp_0'=2,'dp_1'=4,'dp_2'=2,'seq_0'=2,'seq_1'=8] {'seq_0'}, use_global_device_ids=true, to_apply=%add | all-reduce | flops 2 | bytes 16
  133.6 61.1 %all-reduce.1 = s32[16]{0:T(128)S(1)} all-reduce(s32[16]{0:T(128)S(1)} %dynamic-update-slice.1), channel_id=3, replica_groups=mesh['dp_0'=2,'dp_1'=4,'dp_2'=2,'seq_0'=2,'seq_1'=8] {'seq_1'}, use_global_device_ids=true, to_apply=%add.1 | all-reduce | flops 16 | bytes 128
  194.9 40.4 %reduce-scatter.4.cloned.1.call-done = f32[80,1280]{1,0:T(8,128)} async-done(((f32[1280,1280]{1,0:T(8,128)}), f32[80,1280]{1,0:T(8,128)}) %reduce-scatter.4.cloned.1.call-update) | async-done | bytes 409616 | tf_op jit(solution)/shard_map/reduce_scatter | solution.py:109
  235.3 1.7 convert_element_type.54
  237.8 0.9 copy-done.8
  238.7 50.4 %while.11 = (s32[]{:T(128)}, bf16[8,512,1,80]{1,3,2,0:T(8,128)(2,1)S(1)}, bf16[8,512,1,80]{1,3,2,0:T(8,128)(2,1)S(1)}, bf16[4096,1,80]{0,2,1:T(8,128)(2,1)S(1)},...) while((s32[]{:T(128)}, bf16[8,512,1,80]{1,3,2,0:T(8,128)(2,1)S(1)}, ...), condition=%wide.region_5.6_spmd.clone, body=%wide.region_2.5_spmd.clone.sunk | while | flops 696298496 | bytes 26675348 | solution.py:73
  238.8 1.5 fusion.37
  240.3 2.2 fusion.38
  242.5 2.5 fusion.39
  245.1 1.5 fusion.37
  246.6 2.2 fusion.38
  248.8 2.5 fusion.39
  251.4 1.5 fusion.37
  252.9 2.2 fusion.38
  255.1 2.5 fusion.39
  257.7 1.5 fusion.37
  259.2 2.2 fusion.38
  261.4 2.5 fusion.39
  264.0 1.5 fusion.37
  265.5 2.2 fusion.38
  267.7 2.5 fusion.39
  270.3 1.5 fusion.37
  271.8 2.2 fusion.38
  274.0 2.5 fusion.39
  276.6 1.5 fusion.37
  278.1 2.2 fusion.38
  280.3 2.5 fusion.39
  282.9 1.5 fusion.37
  284.4 2.2 fusion.38
  286.6 2.5 fusion.39
  289.7 1.0 copy.42
  290.7 7.2 %all-to-all-start.1 = ((bf16[16,256,80]{1,2,0:T(8,128)(2,1)}), bf16[16,256,80]{1,2,0:T(8,128)(2,1)S(1)}, u32[]{:S(2)}, u32[]{:S(2)}) async-start(bf16[16,256,80]{1,2,0:T(8,128)(2,1)} %copy.42), calls=%async_computation.1 | async-start | bytes 1310720 | tf_op jit(solution)/shard_map/all_to_all | solution.py:98
  297.9 4.0 %copy.43 = bf16[2,4,2,80,1280]{4,3,2,1,0:T(8,128)(2,1)} copy(bf16[2,4,2,80,1280]{4,3,0,1,2:T(8,128)(2,1)} %bitcast.95) | data formatting | bytes 6553600 | tf_op jit(solution)/shard_map/transpose | solution.py:25
  301.9 40.0 %all-gather.17.cloned.1.call-done = bf16[1280,1280]{1,0:T(8,128)(2,1)} async-done(((bf16[80,1280]{1,0:T(8,128)(2,1)}), bf16[1280,1280]{1,0:T(8,128)(2,1)}) %all-gather.17.cloned.1.call-update) | async-done | bytes 3276816 | tf_op jit(solution)/shard_map/all_gather | solution.py:34
  341.9 3.2 convert_reduce_fusion
  345.1 3.9 %fusion.18 = bf16[1,256,1280]{2,1,0:T(8,128)(2,1)} fusion(bf16[256,1280]{0,1:T(8,128)(2,1)S(1)} %bitcast.102, bf16[1280,1280]{1,0:T(8,128)(2,1)} %bitcast.97, f32[256,640]{1,0:T(8,128)S(1)} %copy-done.5, f32[256,640]{1,0:T(8,128)S(1)} %copy-done.3, bf16[1,256,1280]{2,1,0:T(8,128)(2,1)S(1)} %copy-done.7), kind=kOutput, calls=%fused_computation.25 | convolution fusion | flops 840499200 | bytes 6553600 | tf_op jit(solution)/shard_map/dot_general | solution.py:100
  (73 shorter events, 5.1 us)
Async XLA Ops:
  7.2 12.4 %copy-start = (bf16[1,256,1280]{2,1,0:T(8,128)(2,1)S(1)}, bf16[1,256,1280]{2,1,0:T(8,128)(2,1)}, u32[]{:S(2)}) copy-start(bf16[1,256,1280]{2,1,0:T(8,128)(2,1)} %param.15) | copy-start | bytes 1966084
  7.2 88.6 %all-gather.11.cloned.1.call-start = ((), (), s32[]{:S(2)}) async-start(), calls=%async_computation.3 | async-start | bytes 10444800 | tf_op jit(solution)/shard_map/all_gather | solution.py:88
  7.9 117.3 %all-gather.13.cloned.1.call-start = ((), (), s32[]{:S(2)}) async-start(), calls=%async_computation.4 | async-start | bytes 2048000 | tf_op jit(solution)/shard_map/all_gather | solution.py:22
  18.9 216.5 %reduce-scatter.4.cloned.1.call-start = ((), (), s32[]{:S(2)}) async-start(), calls=%async_computation.7 | async-start | bytes 6963200 | tf_op jit(solution)/shard_map/reduce_scatter | solution.py:109
  32.9 0.7 copy-start.9
  32.9 3.1 copy-start.6
  35.9 59.9 %copy-start.4 = (f32[256,640]{1,0:T(8,128)}, f32[256,640]{1,0:T(8,128)S(1)}, u32[]{:S(2)}) copy-start(f32[256,640]{1,0:T(8,128)S(1)} %get-tuple-element.86) | copy-start | bytes 1966084
  35.9 67.7 %copy-start.2 = (f32[256,640]{1,0:T(8,128)}, f32[256,640]{1,0:T(8,128)S(1)}, u32[]{:S(2)}) copy-start(f32[256,640]{1,0:T(8,128)S(1)} %get-tuple-element.85) | copy-start | bytes 1966084
  117.6 8.6 %copy-start.11 = (u32[256]{0:T(256)S(1)}, u32[256]{0:T(256)}, u32[]{:S(2)}) copy-start(u32[256]{0:T(256)} %constant.42) | copy-start | bytes 3076
  117.6 14.5 %copy-start.10 = (u32[256]{0:T(256)S(1)}, u32[256]{0:T(256)}, u32[]{:S(2)}) copy-start(u32[256]{0:T(256)} %constant.47) | copy-start | bytes 3076
  117.6 119.5 %all-to-all-start = ((bf16[256,3,1280]{0,1,2:T(4,128)(2,1)}), bf16[256,3,1280]{0,1,2:T(4,128)(2,1)S(1)}, u32[]{:S(2)}, u32[]{:S(2)}) async-start(bf16[256,3,1280]{0,1,2:T(4,128)(2,1)} %copy.36), calls=%async_computation | async-start | bytes 5242880 | tf_op jit(solution)/shard_map/all_to_all | solution.py:94
  124.8 173.1 %all-gather.15.cloned.1.call-start = ((), (), s32[]{:S(2)}) async-start(), calls=%async_computation.5 | async-start | bytes 4915200 | tf_op jit(solution)/shard_map/all_gather | solution.py:22
  125.4 216.5 %all-gather.17.cloned.1.call-start = ((), (), s32[]{:S(2)}) async-start(), calls=%async_computation.6 | async-start | bytes 3481600 | tf_op jit(solution)/shard_map/all_gather | solution.py:34
  237.6 1.1 copy-start.8
  290.7 54.4 %all-to-all-start.1 = ((bf16[16,256,80]{1,2,0:T(8,128)(2,1)}), bf16[16,256,80]{1,2,0:T(8,128)(2,1)S(1)}, u32[]{:S(2)}, u32[]{:S(2)}) async-start(bf16[16,256,80]{1,2,0:T(8,128)(2,1)} %copy.42), calls=%async_computation.1 | async-start | bytes 1310720 | tf_op jit(solution)/shard_map/all_to_all | solution.py:98
  301.9 43.2 %copy-start.3 = (f32[256,640]{1,0:T(8,128)S(1)}, f32[256,640]{1,0:T(8,128)}, u32[]{:S(2)}) copy-start(f32[256,640]{1,0:T(8,128)} %copy-done.2) | copy-start | bytes 1966084
  301.9 43.2 %copy-start.5 = (f32[256,640]{1,0:T(8,128)S(1)}, f32[256,640]{1,0:T(8,128)}, u32[]{:S(2)}) copy-start(f32[256,640]{1,0:T(8,128)} %copy-done.4) | copy-start | bytes 1966084
  301.9 43.2 %copy-start.7 = (bf16[1,256,1280]{2,1,0:T(8,128)(2,1)S(1)}, bf16[1,256,1280]{2,1,0:T(8,128)(2,1)}, u32[]{:S(2)}) copy-start(bf16[1,256,1280]{2,1,0:T(8,128)(2,1)} %param.10) | copy-start | bytes 1966084
  345.1 3.9 %copy-start.1 = (bf16[1,256,1280]{2,1,0:T(8,128)(2,1)S(1)}, bf16[1,256,1280]{2,1,0:T(8,128)(2,1)}, u32[]{:S(2)}) copy-start(bf16[1,256,1280]{2,1,0:T(8,128)(2,1)} %param.15) | copy-start | bytes 1966084
Sparse Core Ops, SparseCore 0:
  10.7 85.0 all-gather.10
  97.6 27.6 all-gather.12
  129.7 105.5 reduce-scatter.3
  237.0 18.0 all-gather.14
  257.3 84.5 all-gather.16
where the time goes:
time: 356 us
  waiting for transfers between devices  141 us (40%)
  blocking collectives  76.5 us (21%)
  matrix products  48.9 us (14%)
  local copies, waits for them, and re-layouts  32.7 us (9%)
  other arithmetic  25.7 us (7%)
  between operations  15.9 us (4%)
  starting transfers between devices  14.6 us (4%)
    unnamed x2, blocking collectives  65.6 us
    all_gather x1, waiting for transfers between devices, on_device(): lax.all_gather(qkv_weight, DP, axis=0, tiled=True)  59.3 us
    reduce_scatter x1, waiting for transfers between devices, on_device(): lax.psum_scatter(lax.dot_general(column_part, masked_cot, (((0,), (0,)),...  40.4 us
    all_gather x1, waiting for transfers between devices, over_pieces(): return lax.all_gather(x, axis).astype(jnp.float32).sum(0)  40 us
    dot_general x8, matrix products, one_block(): jnp.einsum('hqk,khd->qhd', weights, value_rows, preferred_element_type=jn...  19.9 us
    reduce_sum x8, other arithmetic, one_block(): jnp.sum(exponent, axis=2, keepdims=True)  17.3 us
    dot_general x8, matrix products, one_block(): jnp.einsum('qhd,khd->hqk', block_query, key_rows, preferred_element_type=...  12.3 us
    unnamed x31, local copies, waits for them, and re-layouts  12.1 us
  transfers between devices with their start and end apart: 7, of which 4 were waited for; matrix products, arithmetic and copies ran while one was open for 29% of the time, Pallas kernels for 0%

commit v1 on v0

--- a/solution.py
+++ b/solution.py
@@ -8,6 +8,11 @@
 HEADS = 16
 SEQ = ("seq_0", "seq_1")
 DP = ("dp_0", "dp_1", "dp_2")
+
+
+def swapped_in(x, axis, d):
+    stack = jnp.stack([x] * lax.axis_size(axis))
+    return jnp.concatenate(lax.all_to_all(stack, axis, 0, 0), axis=d)
 
 
 def in_order(parts, dim):
@@ -84,9 +89,7 @@
     normed = layer_norm(with_pos).astype(jnp.bfloat16)
     columns = normed
     projected = jnp.dot(
-        columns,
-        lax.all_gather(qkv_weight, DP, axis=0, tiled=True),
-        preferred_element_type=jnp.float32,
+        columns, swapped_in(qkv_weight, DP, 0), preferred_element_type=jnp.float32
     ).astype(jnp.bfloat16)
     all_counts = gathered_by_axis(counts, SEQ, (0, 1), 1)
     slot_ids = lax.broadcasted_iota(jnp.int32, (1, slot_cap), 1)

time: 356 us -> 374 us (1.051)
  local copies, waits for them, and re-layouts: 32.7 us -> 38.7 us
  starting transfers between devices: 14.6 us -> 19.1 us
    all_to_all x0 -> x1, waiting for transfers between devices: none -> 122 us  [swapped_in(): return jnp.concatenate(lax.all_to_all(stack, axis, 0, 0), axis=d)]
    all_gather x1 -> x0, waiting for transfers between devices: 59.3 us -> none  [on_device(): lax.all_gather(qkv_weight, DP, axis=0, tiled=True)]
    reduce_scatter x1, waiting for transfers between devices: 40.4 us -> 0.01 us  [on_device(): lax.psum_scatter(lax.dot_general(column_part, masked_cot, (((0,), (0,)),...]
    all_gather x1, waiting for transfers between devices: 40 us -> 1.87 us  [over_pieces(): return lax.all_gather(x, axis).astype(jnp.float32).sum(0)]
    all_to_all x1, waiting for transfers between devices: 0.01 us -> 17.8 us  [on_device(): lax.all_to_all(head_context, SEQ, split_axis=0, concat_axis=1, tiled=True)]
    all_to_all x0 -> x1, starting transfers between devices: none -> 6.03 us  [swapped_in(): return jnp.concatenate(lax.all_to_all(stack, axis, 0, 0), axis=d)]
    another operation x0 -> x1, local copies, waits for them, and re-layouts: none -> 5.47 us  [swapped_in(): stack = jnp.stack([x] * lax.axis_size(axis))]
    unnamed x31 -> x33, local copies, waits for them, and re-layouts: 12.1 us -> 12.5 us
  transfers between devices with their start and end apart: 7 -> 7, of which waited for: 4 -> 3; matrix products, arithmetic and copies ran while one was open for 29% -> 29% of each run, Pallas kernels for 0% -> 0%
where the time goes in v1:
time: 374 us; the launch traced here: 371 us
  waiting for transfers between devices  143 us (38%)
  blocking collectives  76.6 us (20%)
  matrix products  47.9 us (13%)
  local copies, waits for them, and re-layouts  38.7 us (10%)
  other arithmetic  28.1 us (8%)
  starting transfers between devices  19.1 us (5%)
  between operations  17.4 us (5%)
    all_to_all x1, waiting for transfers between devices, swapped_in(): return jnp.concatenate(lax.all_to_all(stack, axis, 0, 0), axis=d)  122 us
    unnamed x2, blocking collectives  65.6 us
    dot_general x8, matrix products, one_block(): jnp.einsum('hqk,khd->qhd', weights, value_rows, preferred_element_type=jn...  19.9 us
    all_to_all x1, waiting for transfers between devices, on_device(): lax.all_to_all(head_context, SEQ, split_axis=0, concat_axis=1, tiled=True)  17.8 us
    reduce_sum x8, other arithmetic, one_block(): jnp.sum(exponent, axis=2, keepdims=True)  17.3 us
    unnamed x33, local copies, waits for them, and re-layouts  12.5 us
    dot_general x8, matrix products, one_block(): jnp.einsum('qhd,khd->hqk', block_query, key_rows, preferred_element_type=...  12.3 us
    reshape x1, local copies, waits for them, and re-layouts, on_device(): projected.reshape(slot_cap, 3, model_width)  11.4 us
  transfers between devices with their start and end apart: 7, of which 3 were waited for; matrix products, arithmetic and copies ran while one was open for 29% of the time, Pallas kernels for 0%

profile of v1, /device:TPU:4, one launch (start us, length us, event | category | flops | bytes accessed | tf_op | source)
XLA Modules:
  0.0 370.8 jit_solution(2713881374877188662)
XLA Ops:
  8.1 11.0 %all-gather.2 = bf16[160,1280]{1,0:T(8,128)(2,1)} all-gather(bf16[80,1280]{1,0:T(8,128)(2,1)} %param.14), channel_id=4, replica_groups=mesh['dp_0'=2,'dp_1'=4,'dp_2'=2,'seq_0'=2,'seq_1'=8] {'dp_0'}, dimensions={0}, use_global_device_ids=true | all-gather | bytes 614400 | tf_op jit(solution)/shard_map/all_gather | solution.py:27
  19.1 5.5 %stack.2 = bf16[16,80,3840]{2,1,0:T(8,128)(2,1)} broadcast(bf16[80,3840]{1,0:T(8,128)(2,1)} %param.13), dimensions={1,2} | broadcast | bytes 10444800 | tf_op jit(solution)/shard_map/stack | solution.py:14
  24.5 6.0 %all-to-all-start = ((bf16[16,80,3840]{2,1,0:T(8,128)(2,1)}), bf16[16,80,3840]{2,1,0:T(8,128)(2,1)}, u32[]{:S(2)}, u32[]{:S(2)}) async-start(bf16[16,80,3840]{2,1,0:T(8,128)(2,1)} %stack.2), calls=%async_computation | async-start | bytes 19660800 | tf_op jit(solution)/shard_map/all_to_all | solution.py:15
  31.3 3.9 %fusion.16 = f32[1280,1280]{0,1:T(8,128)} fusion(bf16[1,256,1280]{2,1,0:T(8,128)(2,1)S(1)} %copy-done, bf16[1,256,1280]{2,1,0:T(8,128)(2,1)S(1)} %copy-done.8, pred[256]{0:T(512)(128)(4,1)S(1)} %iota_compare_fusion.1), kind=kOutput, calls=%fused_computation.20 | convolution fusion | flops 840826880 | bytes 7864576 | tf_op jit(solution)/shard_map/dot_general | solution.py:113
  35.2 8.2 %copy.45 = f32[1280,1280]{1,0:T(8,128)} copy(f32[1280,1280]{0,1:T(8,128)} %fusion.16) | data formatting | bytes 13107200
  44.1 2.3 multiply_sine_fusion.1
  47.6 2.3 multiply_sine_fusion
  50.0 122.3 %all-to-all-done = bf16[16,80,3840]{2,1,0:T(8,128)(2,1)} async-done(((bf16[16,80,3840]{2,1,0:T(8,128)(2,1)}), bf16[16,80,3840]{2,1,0:T(8,128)(2,1)}, u32[]{:S(2)}, u32[]{:S(2)}) %all-to-all-start) | async-done | bytes 9830432 | tf_op jit(solution)/shard_map/all_to_all | solution.py:15
  172.4 7.9 %convolution_convert_fusion = bf16[256,3840]{1,0:T(8,128)(2,1)} fusion(bf16[1280,3840]{1,0:T(8,128)(2,1)} %bitcast.3, f32[1,256,640]{2,1,0:T(8,128)S(1)} %get-tuple-element.88, f32[1,256,640]{2,1,0:T(8,128)S(1)} %get-tuple-element.87, bf16[1,256,1280]{2,1,0:T(8,128)(2,1)S(1)} %copy-done.6, f32[256]{0:T(256)S(1)} %add_rsqrt_fusion, ...), kind=kOutput, calls=%fused_computation.22 | convolution fusion | flops 2519531520 | bytes 13764608 | tf_op jit(solution)/shard_map/dot_general | solution.py:91
  180.2 2.7 copy.35
  182.9 11.4 %copy.36 = bf16[256,3,1280]{0,1,2:T(4,128)(2,1)} copy(bf16[256,3,1280]{0,2,1:T(8,128)(2,1)S(1)} %bitcast.95) | data formatting | bytes 3932160 | tf_op jit(solution)/shard_map/reshape | solution.py:98
  194.3 9.2 %all-to-all-start.1 = ((bf16[256,3,1280]{0,1,2:T(4,128)(2,1)}), bf16[256,3,1280]{0,1,2:T(4,128)(2,1)S(1)}, u32[]{:S(2)}, u32[]{:S(2)}) async-start(bf16[256,3,1280]{0,1,2:T(4,128)(2,1)} %copy.36), calls=%async_computation.1 | async-start | bytes 5242880 | tf_op jit(solution)/shard_map/all_to_all | solution.py:97
  206.2 4.6 %all-reduce = s32[2]{0:T(128)S(1)} all-reduce(s32[2]{0:T(128)S(1)} %bitcast_dynamic-update-slice_fusion), channel_id=2, replica_groups=mesh['dp_0'=2,'dp_1'=4,'dp_2'=2,'seq_0'=2,'seq_1'=8] {'seq_0'}, use_global_device_ids=true, to_apply=%add | all-reduce | flops 2 | bytes 16
  212.3 61.1 %all-reduce.1 = s32[16]{0:T(128)S(1)} all-reduce(s32[16]{0:T(128)S(1)} %dynamic-update-slice.1), channel_id=3, replica_groups=mesh['dp_0'=2,'dp_1'=4,'dp_2'=2,'seq_0'=2,'seq_1'=8] {'seq_1'}, use_global_device_ids=true, to_apply=%add.1 | all-reduce | flops 16 | bytes 128
  273.6 1.7 convert_element_type.62
  276.1 0.9 copy-done.9
  277.0 50.4 %while.11 = (s32[]{:T(128)}, bf16[8,512,1,80]{1,3,2,0:T(8,128)(2,1)S(1)}, bf16[8,512,1,80]{1,3,2,0:T(8,128)(2,1)S(1)}, bf16[4096,1,80]{0,2,1:T(8,128)(2,1)S(1)},...) while((s32[]{:T(128)}, bf16[8,512,1,80]{1,3,2,0:T(8,128)(2,1)S(1)}, ...), condition=%wide.region_5.6_spmd.clone, body=%wide.region_2.5_spmd.clone.sunk | while | flops 696298496 | bytes 26675356 | solution.py:78
  277.1 1.5 fusion.44
  278.6 2.2 fusion.45
  280.8 2.5 fusion.46
  283.4 1.5 fusion.44
  284.9 2.2 fusion.45
  287.1 2.5 fusion.46
  289.7 1.5 fusion.44
  291.2 2.2 fusion.45
  293.4 2.5 fusion.46
  296.0 1.5 fusion.44
  297.5 2.2 fusion.45
  299.7 2.5 fusion.46
  302.3 1.5 fusion.44
  303.8 2.2 fusion.45
  306.0 2.5 fusion.46
  308.6 1.5 fusion.44
  310.1 2.2 fusion.45
  312.3 2.5 fusion.46
  314.9 1.5 fusion.44
  316.4 2.2 fusion.45
  318.6 2.5 fusion.46
  321.2 1.5 fusion.44
  322.7 2.2 fusion.45
  324.9 2.5 fusion.46
  328.0 1.0 copy.42
  329.0 3.8 %all-to-all-start.2 = ((bf16[16,256,80]{1,2,0:T(8,128)(2,1)}), bf16[16,256,80]{1,2,0:T(8,128)(2,1)S(1)}, u32[]{:S(2)}, u32[]{:S(2)}) async-start(bf16[16,256,80]{1,2,0:T(8,128)(2,1)} %copy.42), calls=%async_computation.2 | async-start | bytes 1310720 | tf_op jit(solution)/shard_map/all_to_all | solution.py:101
  332.9 4.1 %copy.43 = bf16[2,4,2,80,1280]{4,3,2,1,0:T(8,128)(2,1)} copy(bf16[2,4,2,80,1280]{4,3,0,1,2:T(8,128)(2,1)} %bitcast.97) | data formatting | bytes 6553600 | tf_op jit(solution)/shard_map/transpose | solution.py:30
  336.9 17.8 %all-to-all-done.2 = bf16[16,256,80]{1,2,0:T(8,128)(2,1)S(1)} async-done(((bf16[16,256,80]{1,2,0:T(8,128)(2,1)}), bf16[16,256,80]{1,2,0:T(8,128)(2,1)S(1)}, u32[]{:S(2)}, u32[]{:S(2)}) %all-to-all-start.2) | async-done | bytes 655392 | tf_op jit(solution)/shard_map/all_to_all | solution.py:101
  354.7 3.9 %fusion.18 = bf16[1,256,1280]{2,1,0:T(8,128)(2,1)} fusion(bf16[256,1280]{0,1:T(8,128)(2,1)S(1)} %bitcast.104, bf16[1280,1280]{1,0:T(8,128)(2,1)} %bitcast.99, f32[256,640]{1,0:T(8,128)S(1)} %copy-done.5, f32[256,640]{1,0:T(8,128)S(1)} %copy-done.3, bf16[1,256,1280]{2,1,0:T(8,128)(2,1)S(1)} %copy-done.7), kind=kOutput, calls=%fused_computation.25 | convolution fusion | flops 840499200 | bytes 6553600 | tf_op jit(solution)/shard_map/dot_general | solution.py:103
  358.6 1.9 all-gather.14.cloned.1.call-done
  360.5 3.2 convert_reduce_fusion
  (76 shorter events, 7.1 us)
Async XLA Ops:
  8.0 23.3 %copy-start = (bf16[1,256,1280]{2,1,0:T(8,128)(2,1)S(1)}, bf16[1,256,1280]{2,1,0:T(8,128)(2,1)}, u32[]{:S(2)}) copy-start(bf16[1,256,1280]{2,1,0:T(8,128)(2,1)} %param.15) | copy-start | bytes 1966084
  8.0 195.6 %all-gather.10.cloned.1.call-start = ((), (), s32[]{:S(2)}) async-start(), calls=%async_computation.4 | async-start | bytes 2048000 | tf_op jit(solution)/shard_map/all_gather | solution.py:27
  24.5 6.7 %copy-start.8 = (bf16[1,256,1280]{2,1,0:T(8,128)(2,1)S(1)}, bf16[1,256,1280]{2,1,0:T(8,128)(2,1)}, u32[]{:S(2)}) copy-start(bf16[1,256,1280]{2,1,0:T(8,128)(2,1)} %param.16) | copy-start | bytes 1966084
  24.5 147.8 %all-to-all-start = ((bf16[16,80,3840]{2,1,0:T(8,128)(2,1)}), bf16[16,80,3840]{2,1,0:T(8,128)(2,1)}, u32[]{:S(2)}, u32[]{:S(2)}) async-start(bf16[16,80,3840]{2,1,0:T(8,128)(2,1)} %stack.2), calls=%async_computation | async-start | bytes 19660800 | tf_op jit(solution)/shard_map/all_to_all | solution.py:15
  30.6 243.0 %reduce-scatter.4.cloned.1.call-start = ((), (), s32[]{:S(2)}) async-start(), calls=%async_computation.7 | async-start | bytes 6963200 | tf_op jit(solution)/shard_map/reduce_scatter | solution.py:112
  43.4 0.7 copy-start.10
  43.4 3.1 copy-start.6
  46.5 0.8 copy-start.4
  46.5 133.7 %copy-start.2 = (f32[256,640]{1,0:T(8,128)}, f32[256,640]{1,0:T(8,128)S(1)}, u32[]{:S(2)}) copy-start(f32[256,640]{1,0:T(8,128)S(1)} %get-tuple-element.85) | copy-start | bytes 1966084
  194.3 10.6 %copy-start.12 = (u32[256]{0:T(256)S(1)}, u32[256]{0:T(256)}, u32[]{:S(2)}) copy-start(u32[256]{0:T(256)} %constant.42) | copy-start | bytes 3076
  194.3 16.5 %copy-start.11 = (u32[256]{0:T(256)S(1)}, u32[256]{0:T(256)}, u32[]{:S(2)}) copy-start(u32[256]{0:T(256)} %constant.47) | copy-start | bytes 3076
  194.3 81.0 %all-to-all-start.1 = ((bf16[256,3,1280]{0,1,2:T(4,128)(2,1)}), bf16[256,3,1280]{0,1,2:T(4,128)(2,1)S(1)}, u32[]{:S(2)}, u32[]{:S(2)}) async-start(bf16[256,3,1280]{0,1,2:T(4,128)(2,1)} %copy.36), calls=%async_computation.1 | async-start | bytes 5242880 | tf_op jit(solution)/shard_map/all_to_all | solution.py:97
  203.5 129.3 %all-gather.12.cloned.1.call-start = ((), (), s32[]{:S(2)}) async-start(), calls=%async_computation.5 | async-start | bytes 4915200 | tf_op jit(solution)/shard_map/all_gather | solution.py:27
  204.3 156.3 %all-gather.14.cloned.1.call-start = ((), (), s32[]{:S(2)}) async-start(), calls=%async_computation.6 | async-start | bytes 3481600 | tf_op jit(solution)/shard_map/all_gather | solution.py:39
  275.9 1.1 copy-start.9
  329.0 25.7 %all-to-all-start.2 = ((bf16[16,256,80]{1,2,0:T(8,128)(2,1)}), bf16[16,256,80]{1,2,0:T(8,128)(2,1)S(1)}, u32[]{:S(2)}, u32[]{:S(2)}) async-start(bf16[16,256,80]{1,2,0:T(8,128)(2,1)} %copy.42), calls=%async_computation.2 | async-start | bytes 1310720 | tf_op jit(solution)/shard_map/all_to_all | solution.py:101
  332.8 21.9 %copy-start.3 = (f32[256,640]{1,0:T(8,128)S(1)}, f32[256,640]{1,0:T(8,128)}, u32[]{:S(2)}) copy-start(f32[256,640]{1,0:T(8,128)} %copy-done.2) | copy-start | bytes 1966084
  332.8 21.9 %copy-start.5 = (f32[256,640]{1,0:T(8,128)S(1)}, f32[256,640]{1,0:T(8,128)}, u32[]{:S(2)}) copy-start(f32[256,640]{1,0:T(8,128)} %copy-done.4) | copy-start | bytes 1966084
  332.8 21.9 %copy-start.7 = (bf16[1,256,1280]{2,1,0:T(8,128)(2,1)S(1)}, bf16[1,256,1280]{2,1,0:T(8,128)(2,1)}, u32[]{:S(2)}) copy-start(bf16[1,256,1280]{2,1,0:T(8,128)(2,1)} %param.10) | copy-start | bytes 1966084
  354.7 9.0 %copy-start.1 = (bf16[1,256,1280]{2,1,0:T(8,128)(2,1)S(1)}, bf16[1,256,1280]{2,1,0:T(8,128)(2,1)}, u32[]{:S(2)}) copy-start(bf16[1,256,1280]{2,1,0:T(8,128)(2,1)} %param.15) | copy-start | bytes 1966084
Sparse Core Ops, SparseCore 0:
  19.2 52.8 all-gather.9
  206.1 23.5 all-gather.11
  275.5 85.0 all-gather.13
Sparse Core Ops, SparseCore 1:
  43.5 155.6 reduce-scatter.3
